TPU v7x, 256 devices: a whole 4x4x8 slice. The times are simulated.
256 devices in a mesh: gx: 2 (over core), gy: 2 (over x_lo), gz: 64 (over z, y, x_hi).
Axes of the slice: x: 4 (x_hi: 2, x_lo: 2; x = x_hi * 2 + x_lo), y: 4, z: 8, core: 2. Of those that a mesh axis runs over, the one named last changes fastest.
Arguments:
- old_pos: float32 [3, 262144], P(None, ('gx', 'gy', 'gz')), may hold values from -6 to 6
- new_pos: float32 [3, 262144], P(None, ('gx', 'gy', 'gz')), may hold values from -6 to 6
- inv_mass: float32 [262144], P(('gx', 'gy', 'gz')), may hold values from 0.05 to 1
- rest_length: float32 [262144], P(('gx', 'gy', 'gz')), may hold values from 0.8 to 1.6
- bond_pairs: int32 [2, 262144], P(None, ('gx', 'gy', 'gz')), may hold values from 0 to 1311, as said below
- live: int32 [262144], P(('gx', 'gy', 'gz')), may hold values from 0 to 1, as said below
- send_index: int32 [1536, 48], P(('gx', 'gy', 'gz')), may hold values from 0 to 1023, as said below
Outputs:
- displacement: float32 [3, 262144], P(None, ('gx', 'gy', 'gz'))
- multipliers: float32 [262144], P(('gx', 'gy', 'gz'))
Inputs may be any that keep to these rules, and one draw needn't show every extreme that they name: `bond_pairs`: in domain k's slots, row 0 is an own atom (0 to 1023). Row 1 indexes the domain's extended list: its own atoms, then six blocks of 48 received atoms, block 2a + s holding, in order, list 2a + s of the neighbour one step down (s = 0) or up (s = 1) along axis a. Every atom is in at most two live constraints, each received atom is the second atom of at most one live constraint, and exactly 216 live constraints of each domain name a received atom. `live`: padding slots change nothing. `send_index`: rows 6k to 6k + 5 are domain k's lists of own atoms; list 2a + s goes to the neighbour one step up (s = 0) or down (s = 1) along axis a, periodically. The 288 entries of a domain are distinct.
All inputs are finite; a program needn't handle non-finite values.
Results may differ from a plain program's by a relative error of at most 0.0001.
Values sent between devices are 32-bit elements; how exact they have to be, the bound alone decides.
A program may use at most 64 MiB of HBM per device.

v0:
```python
import jax
import jax.numpy as jnp
from jax import lax
from jax.experimental import pallas as pl
from jax.experimental.pallas import tpu as pltpu
from jax.sharding import PartitionSpec as P

MESH = pl.DeviceIdType.MESH
ORDER = 4
W = 48
F32 = jnp.float32
I32 = jnp.int32
ROUND_FIELDS = (7, 4) + (1,) * 9


def lane_pick(row, lo):
    return jnp.take_along_axis(jnp.broadcast_to(row, (8, 128)), lo, axis=1)


class Index:
    def __init__(self, idx):
        self.lo = idx & 127
        self.hi = idx >> 7

    def look(self, rows, base=0, start=None):
        out = jnp.zeros((8, 128), rows[0].dtype) if start is None else start
        for j, row in enumerate(rows):
            out = jnp.where(self.hi == base + j, lane_pick(row, self.lo), out)
        return out


def rows_of(tile, count=8):
    return [tile[j : j + 1, :] for j in range(count)]


def one_hot_pair(idx_rows, hi_count, values):
    low, high = [], [[] for _ in values]
    for j, row in enumerate(idx_rows):
        lo = jnp.broadcast_to(row & 127, (128, 128))
        low.append(jnp.where(lo == lax.broadcasted_iota(I32, (128, 128), 0), 1.0, 0.0).astype(jnp.bfloat16))
        hit = jnp.broadcast_to(row >> 7, (hi_count, 128)) == lax.broadcasted_iota(I32, (hi_count, 128), 0)
        for k, value in enumerate(values):
            picked = jnp.where(hit, jnp.broadcast_to(value[j], (hi_count, 128)), 0.0)
            high[k].append(picked.astype(jnp.bfloat16))
    return jnp.concatenate(low, 1), [jnp.concatenate(h, 1) for h in high]


def contract(a, b):
    return lax.dot_general(a, b, (((1,), (1,)), ((), ())), preferred_element_type=F32)


def kernel(old_ref, new_ref, mass_ref, rest_ref, pair_ref, live_ref, send_ref, disp_ref, mult_ref, tile_ref, list_ref, *bufs):
    rounds = len(ROUND_FIELDS)
    snd, rcv = bufs[:rounds], bufs[rounds : 2 * rounds]
    ssem, rsem = bufs[2 * rounds], bufs[2 * rounds + 1]
    ix, iy, iz = lax.axis_index("gx"), lax.axis_index("gy"), lax.axis_index("gz")
    nz = lax.axis_size("gz")
    up = lax.rem(iz + 1, nz)
    down = lax.rem(iz + nz - 1, nz)
    peers = [({"gx": 1 - ix}, 0, 2), ({"gy": 1 - iy}, 2, 2), ({"gz": up}, 4, 1), ({"gz": down}, 5, 1)]

    barrier = pltpu.get_barrier_semaphore()
    for device, _, _ in peers:
        pl.semaphore_signal(barrier, inc=1, device_id=device, device_id_type=MESH)

    def send(k, fields):
        for f, field in enumerate(fields):
            for i in range(6):
                snd[k][i, f : f + 1, :] = field[i : i + 1, :]
        copies = []
        for p, (device, row, count) in enumerate(peers):
            copy = pltpu.make_async_remote_copy(
                src_ref=snd[k].at[pl.ds(row, count)],
                dst_ref=rcv[k].at[pl.ds(row, count)],
                send_sem=ssem.at[k, p],
                recv_sem=rsem.at[k, p],
                device_id=device,
                device_id_type=MESH,
            )
            copy.start()
            copies.append(copy)
        return copies

    def arrive(k, copies):
        for copy in copies:
            copy.wait()
        return [[rcv[k][i, f : f + 1, :] for i in range(6)] for f in range(ROUND_FIELDS[k])]

    def tile(n, ref, row):
        for j in range(8):
            tile_ref[n, j : j + 1, :] = ref[row : row + 1, 128 * j : 128 * j + 128]
        return tile_ref[n]

    lane = lax.broadcasted_iota(I32, (8, 128), 1)
    sub = lax.broadcasted_iota(I32, (8, 128), 0)
    slot = sub * 128 + lane

    list_ref[...] = jnp.full((8, 128), -1, I32)
    list_ref[0:6, 0:W] = send_ref[...]
    listed = list_ref[...]
    at_list = Index(listed)
    own = [tile(n, old_ref, n) for n in range(3)] + [tile(3 + n, new_ref, n) for n in range(3)] + [mass_ref[...]]
    own_rows = [rows_of(field) for field in own]
    fields = [at_list.look(field) for field in own_rows]
    pl.semaphore_wait(barrier, 4)
    moving = send(0, fields)

    mass = own[6]
    rest = rest_ref[...]
    alive = live_ref[...] != 0
    pair_rows = [[pair_ref[r : r + 1, 128 * j : 128 * j + 128] for j in range(8)] for r in range(2)]
    for r in range(2):
        for j in range(8):
            list_ref[j : j + 1, :] = pair_rows[r][j]
        if r == 0:
            first = list_ref[...]
        else:
            second = list_ref[...]
    off = second - 1024
    block = jnp.zeros((8, 128), I32)
    for t in range(1, 6):
        block = block + jnp.where(off >= W * t, 1, 0)
    remote = off >= 0
    lane_in = off - W * block
    ghost = 1024 + 128 * block + lane_in
    target = jnp.where(remote, 1024 + 128 * (block ^ 1) + 64 + lane_in, second)
    joins = jnp.logical_and(alive, first != second)
    label = jnp.where(joins, slot + 1, 0)
    v_low = (label & 127).astype(F32)
    v_high = (label >> 7).astype(F32)
    v_high_first = v_high + jnp.where(joins, 32.0, 0.0)
    low_f, (hf1, hf2) = one_hot_pair(rows_of(first), 16, [rows_of(v_low), rows_of(v_high_first)])
    low_s, (hs1, hs2) = one_hot_pair(rows_of(target), 16, [rows_of(v_low), rows_of(v_high)])
    low = jnp.concatenate([low_f, low_s], 1)
    high = jnp.concatenate([jnp.concatenate([hf1, hs1], 1), jnp.concatenate([hf2, hs2], 1)], 0)
    summed = contract(high, low)
    code = (summed[0:16] + 128.0 * summed[16:32]).astype(I32)
    code_rows = rows_of(code)
    owner_ghost = 1024 + 128 * (sub ^ 1) + 64 + lane
    o_low = ((owner_ghost + 1) & 127).astype(F32)
    o_high = ((owner_ghost + 1) >> 7).astype(F32)
    low_l, (hl1, hl2) = one_hot_pair(rows_of(listed, 6), 16, [rows_of(o_low, 6), rows_of(o_high, 6)])
    linked = contract(jnp.concatenate([hl1, hl2], 0), low_l)
    link_rows = rows_of((linked[0:16] + 128.0 * linked[16:32]).astype(I32))

    at_first, at_second = Index(first), Index(second)
    own1 = jnp.where(joins, slot + 1 + 4096, 0)
    own2 = jnp.where(joins, slot + 1, 0)

    def other(at, mine):
        left = at.look(code_rows) - mine
        via_link = at.look(link_rows)
        number = jnp.where(left > 0, (left & 4095) - 1, via_link - 1)
        sign = jnp.where(left >= 4096, 1.0, -1.0)
        return left, number, sign

    left1, n1, sign1 = other(at_first, own1)
    left2, n2, sign2 = other(at_second, own2)
    n2 = jnp.where(remote, ghost, n2)
    at_n1, at_n2 = Index(n1), Index(n2)
    sign1 = jnp.where(n1 >= 1024, 1.0, sign1)
    sign2 = jnp.where(n2 >= 1024, 1.0, sign2)

    face_code = jnp.where(lane < 64, at_list.look(code_rows), code[8:16])
    face_code = jnp.where(sub < 6, face_code, 0)
    face = (face_code & 4095) - 1
    face_sign = jnp.where(face_code >= 4096, 1.0, -1.0)
    at_face = Index(face)

    def at_faces(field):
        return at_face.look(rows_of(field))

    from_first = [at_first.look(field) for field in own_rows]
    from_second = [at_second.look(field) for field in own_rows]
    head1 = jnp.logical_and(joins, jnp.logical_or(left1 <= 0, slot < n1))
    head2 = jnp.logical_and(jnp.logical_and(joins, jnp.logical_not(remote)), jnp.logical_or(left2 <= 0, slot < n2))
    head_values = []
    for head, flag in ((head1, 32.0), (head2, 0.0)):
        head_values.append((jnp.where(head, v_low, 0.0), jnp.where(head, v_high + flag, 0.0)))

    def high_of(idx_rows, value_rows):
        parts = []
        for row, value in zip(idx_rows, value_rows):
            hit = jnp.broadcast_to(row >> 7, (8, 128)) == sub
            parts.append(jnp.where(hit, jnp.broadcast_to(value, (8, 128)), 0.0).astype(jnp.bfloat16))
        return jnp.concatenate(parts, 1)

    heads = [
        jnp.concatenate([high_of(rows_of(first), rows_of(head_values[0][k])), high_of(rows_of(target), rows_of(head_values[1][k]))], 1)
        for k in range(2)
    ]
    headed = contract(jnp.concatenate(heads, 0), low)
    head_code = (headed[0:8] + 128.0 * headed[8:16]).astype(I32)

    ghosts = arrive(0, moving)
    at_ghost = Index(jnp.where(remote, ghost, -1))
    from_second = [at_ghost.look(ghosts[f], 8, from_second[f]) for f in range(7)]
    span = [from_first[f] - from_second[f] for f in range(6)]
    mass1, mass2 = from_first[6], from_second[6]
    scale = jnp.where(alive, 1.0, 0.0) / jnp.sqrt(mass1 + mass2)
    inverse = 1.0 / jnp.sqrt(span[0] * span[0] + span[1] * span[1] + span[2] * span[2] + 0.25)
    unit = [span[n] * inverse for n in range(3)]
    arm = [scale * unit[n] for n in range(3)]
    pull = span[3:6]
    x = scale * (unit[0] * pull[0] + unit[1] * pull[1] + unit[2] * pull[2] - rest)
    moving = send(1, [face_sign * at_faces(arm[n]) for n in range(3)] + [at_faces(x)])

    def dot3(a, b):
        return a[0] * b[0] + a[1] * b[1] + a[2] * b[2]

    mass12 = mass1 + mass2
    diag = 1.0 - dot3(arm, arm) * mass12
    arm_rows = [rows_of(arm[n]) for n in range(3)]
    via1 = [sign1 * at_n1.look(arm_rows[n]) for n in range(3)]
    via2 = [sign2 * at_n2.look(arm_rows[n]) for n in range(3)]

    def near(field):
        rows = rows_of(field)
        return at_n1.look(rows), at_n2.look(rows)

    x1, x2 = near(x)
    ghosts = arrive(1, moving)
    via1 = [mass1 * at_n1.look(ghosts[n], 8, via1[n]) for n in range(3)]
    via2 = [-mass2 * at_n2.look(ghosts[n], 8, via2[n]) for n in range(3)]
    e1 = -dot3(arm, via1)
    e2 = -dot3(arm, via2)
    x1 = at_n1.look(ghosts[3], 8, x1)
    x2 = at_n2.look(ghosts[3], 8, x2)

    k = 2

    def exchange(k, field):
        moving = send(k, [at_faces(field)])
        f1, f2 = near(field)
        ghosts = arrive(k, moving)
        return at_n1.look(ghosts[0], 8, f1), at_n2.look(ghosts[0], 8, f2), ghosts[0]

    def expansion(k, x, x1, x2):
        total = x
        for step in range(ORDER):
            x = diag * x + e1 * x1 + e2 * x2
            total = total + x
            if step < ORDER - 1:
                x1, x2, _ = exchange(k, x)
                k += 1
        return total, k

    y, k = expansion(k, x, x1, x2)
    y1, y2, _ = exchange(k, y)
    k += 1
    stretch = [pull[n] - (mass12 * arm[n] * y + via1[n] * y1 + via2[n] * y2) for n in range(3)]
    square = rest * rest
    goal = jnp.sqrt(jnp.maximum(2.0 * square - dot3(stretch, stretch), 0.25 * square))
    x = scale * (rest - goal)
    x1, x2, _ = exchange(k, x)
    k += 1
    y_second, k = expansion(k, x, x1, x2)
    z = y + y_second
    mult_ref[...] = z

    moving = send(k, [at_faces(z)])
    z_rows = rows_of(z)
    has_head = head_code > 0
    head_first = head_code >= 4096
    head_slot = (head_code & 4095) - 1
    link = jnp.concatenate(link_rows, 0) - 1
    at_head = Index(head_slot)
    next1 = at_head.look(rows_of(n1))
    next2 = at_head.look(rows_of(n2))
    turn = jnp.where(head_first, 1.0, -1.0)
    tail_slot = jnp.where(has_head, jnp.where(head_first, next1, next2), link)
    at_tail = Index(tail_slot)
    tail_sign = jnp.where(
        head_first, at_head.look(rows_of(sign1)), at_head.look(rows_of(sign2))
    )
    arm_head = [turn * at_head.look(arm_rows[n]) for n in range(3)]
    arm_tail = [at_tail.look(ghosts[n], 8, tail_sign * at_tail.look(arm_rows[n])) for n in range(3)]
    z_head = at_head.look(z_rows)
    z_tail = at_tail.look(z_rows)
    last = arrive(k, moving)
    z_tail = at_tail.look(last[0], 8, z_tail)
    for n in range(3):
        moved = -mass * (arm_head[n] * z_head + arm_tail[n] * z_tail)
        for j in range(8):
            disp_ref[n : n + 1, 128 * j : 128 * j + 128] = moved[j : j + 1, :]


def per_device(old_pos, new_pos, inv_mass, rest_length, bond_pairs, live, send_index):
    vmem = pl.BlockSpec(memory_space=pltpu.VMEM)
    rounds = len(ROUND_FIELDS)
    faces = [pltpu.VMEM((6, f, 128), F32) for f in ROUND_FIELDS]
    disp, mult = pl.pallas_call(
        kernel,
        out_shape=(jax.ShapeDtypeStruct((3, 1024), F32), jax.ShapeDtypeStruct((8, 128), F32)),
        in_specs=[vmem] * 7,
        out_specs=(vmem, vmem),
        scratch_shapes=[pltpu.VMEM((6, 8, 128), F32), pltpu.VMEM((8, 128), I32)]
        + faces
        + faces
        + [pltpu.SemaphoreType.DMA((rounds, 4)), pltpu.SemaphoreType.DMA((rounds, 4))],
        compiler_params=pltpu.CompilerParams(collective_id=0, has_side_effects=True),
        name="plincs",
    )(
        old_pos,
        new_pos,
        inv_mass.reshape(8, 128),
        rest_length.reshape(8, 128),
        bond_pairs,
        live.reshape(8, 128),
        send_index,
    )
    return disp, mult.reshape(1024)


def solution(mesh):
    in_specs = (
        P(None, ("gx", "gy", "gz")),
        P(None, ("gx", "gy", "gz")),
        P(("gx", "gy", "gz")),
        P(("gx", "gy", "gz")),
        P(None, ("gx", "gy", "gz")),
        P(("gx", "gy", "gz")),
        P(("gx", "gy", "gz"), None),
    )
    out_specs = (P(None, ("gx", "gy", "gz")), P(("gx", "gy", "gz")))
    return jax.shard_map(
        per_device, mesh=mesh, in_specs=in_specs, out_specs=out_specs, check_vma=False
    )
```

profile of v0, /device:TPU:1, one launch (start us, length us, event | category | flops | bytes accessed | tf_op | source)
XLA Modules:
  0.0 74.1 jit_solution(7544831420187193980)
XLA Ops:
  0.6 71.5 %plincs.1 = (f32[3,1024]{1,0:T(4,128)}, f32[8,128]{1,0:T(8,128)}) custom-call(f32[3,1024]{1,0:T(4,128)} %old_ref.1, f32[3,1024]{1,0:T(4,128)} %new_ref.1, f32[8,128]{1,0:T(8,128)} %bitcast.4, f32[8,128]{1,0:T(8,128)} %bitcast.5, s32[2,1024]{1,0:T(2,128)} %pair_ref.1, s32[8,128]{1,0:T(8,128)} %bitcast.6, s32[6,48]{1,0:T(8,128)} %send_ref.1), custom_call_target="tpu_custom_call" | custom-call | tf_op jit(solution)/shard_map/plincs/pallas_call | solution.py:292
  72.2 0.0 copy-start
  72.2 1.3 %copy.11 = f32[3,1024]{1,0:T(4,128)} copy(f32[3,1024]{1,0:T(4,128)} %get-tuple-element.8) | data formatting | bytes 24576
  73.5 0.0 copy-done
  73.5 0.6 copy.12
Async XLA Ops:
  72.2 1.3 %copy-start = (f32[8,128]{1,0:T(8,128)S(1)}, f32[8,128]{1,0:T(8,128)}, u32[]{:S(2)}) copy-start(f32[8,128]{1,0:T(8,128)} %get-tuple-element.5) | copy-start | bytes 12292
where the time goes:
time: 74.3 us; the launch traced here: 74.1 us
  Pallas kernels  71.5 us (96%)
  local copies, waits for them, and re-layouts  1.92 us (3%)
    pallas_call x1, Pallas kernels, per_device(): pl.pallas_call(kernel, out_shape=(jax.ShapeDtypeStruct((3, 1024), F32), j...  71.5 us
    unnamed x4, local copies, waits for them, and re-layouts  1.92 us

commit v1 on v0

--- a/solution.py
+++ b/solution.py
@@ -10,7 +10,67 @@
 W = 48
 F32 = jnp.float32
 I32 = jnp.int32
-ROUND_FIELDS = (7, 4) + (1,) * 9
+FIRST_PLAN = (3,)
+SECOND_PLAN = (5,)
+DEEP = max(FIRST_PLAN + SECOND_PLAN)
+LIST_ROW = (0, 1, 4, 5, 2, 3)
+STEPS = ((1, 0, 0), (1, 0, 0), (0, 0, -1), (0, 0, 1), (0, 1, 0), (0, 1, 0))
+
+
+def moved_by(o, i, turn=1):
+    s = STEPS[i]
+    return ((o[0] + s[0]) % 2, (o[1] + s[1]) % 2, o[2] + turn * s[2])
+
+
+def dist(o):
+    return o[0] + o[1] + abs(o[2])
+
+
+def offsets(depth):
+    every = [(x, y, z) for x in range(2) for y in range(2) for z in range(-depth, depth + 1)]
+    return [o for o in every if 0 < dist(o) <= depth]
+
+
+def blocks(depth, levels=None):
+    out = []
+    for o in offsets(depth):
+        need = [max(0, depth - dist(moved_by(o, i, -1))) for i in range(6)]
+        if levels is not None:
+            need = [min(n, levels) for n in need]
+        i = 0
+        while i < 6:
+            j = i
+            while j < 6 and need[j] == need[i]:
+                j += 1
+            if need[i]:
+                out.append((o, need[i], i, j - i))
+            i = j
+    return out
+
+
+class Plan:
+    def __init__(self, depth, fields, levels=None):
+        self.depth, self.fields = depth, fields
+        self.levels = depth if levels is None else levels
+        self.blocks = blocks(depth, levels)
+        self.offsets = offsets(depth)
+
+    def shapes(self):
+        box = (self.levels, 6, self.fields, 128)
+        return [
+            pltpu.VMEM(box, F32),
+            pltpu.VMEM((len(self.offsets),) + box, F32),
+            pltpu.SemaphoreType.DMA((len(self.blocks),)),
+            pltpu.SemaphoreType.DMA((len(self.blocks),)),
+        ]
+
+
+def plans():
+    out = [Plan(1, 7), Plan(DEEP - 1, 1, 1), Plan(1, 4), Plan(max(FIRST_PLAN) - 1, 2)]
+    out += [Plan(d, 1) for d in FIRST_PLAN]
+    out += [Plan(max(SECOND_PLAN) - 1, 2), Plan(1, 1)]
+    out += [Plan(d, 1) for d in SECOND_PLAN]
+    return out
 
 
 def lane_pick(row, lo):
@@ -49,42 +109,88 @@
     return lax.dot_general(a, b, (((1,), (1,)), ((), ())), preferred_element_type=F32)
 
 
-def kernel(old_ref, new_ref, mass_ref, rest_ref, pair_ref, live_ref, send_ref, disp_ref, mult_ref, tile_ref, list_ref, *bufs):
-    rounds = len(ROUND_FIELDS)
-    snd, rcv = bufs[:rounds], bufs[rounds : 2 * rounds]
-    ssem, rsem = bufs[2 * rounds], bufs[2 * rounds + 1]
+def kernel(old_ref, new_ref, mass_ref, rest_ref, pair_ref, live_ref, send_ref, disp_ref, mult_ref, tile_ref, list_ref, pile_ref, *bufs):
     ix, iy, iz = lax.axis_index("gx"), lax.axis_index("gy"), lax.axis_index("gz")
     nz = lax.axis_size("gz")
-    up = lax.rem(iz + 1, nz)
-    down = lax.rem(iz + nz - 1, nz)
-    peers = [({"gx": 1 - ix}, 0, 2), ({"gy": 1 - iy}, 2, 2), ({"gz": up}, 4, 1), ({"gz": down}, 5, 1)]
+
+    def peer(o):
+        device = {}
+        if o[0]:
+            device["gx"] = 1 - ix
+        if o[1]:
+            device["gy"] = 1 - iy
+        if o[2]:
+            device["gz"] = lax.rem(iz + nz - o[2], nz)
+        return device
 
     barrier = pltpu.get_barrier_semaphore()
-    for device, _, _ in peers:
-        pl.semaphore_signal(barrier, inc=1, device_id=device, device_id_type=MESH)
-
-    def send(k, fields):
-        for f, field in enumerate(fields):
+    for o in offsets(DEEP):
+        pl.semaphore_signal(barrier, inc=1, device_id=peer(o), device_id_type=MESH)
+
+    todo = plans()
+
+    count = {"tile": 6, "pile": 0}
+
+    def fresh(name, ref, low=0):
+        n = count[name]
+        count[name] = n + 1 if n + 1 < ref.shape[0] else low
+        return ref.at[n]
+
+    class Exchange:
+        def __init__(self, number, levels):
+            self.plan = plan = todo[number]
+            self.out, self.box, ssem, rsem = bufs[4 * number : 4 * number + 4]
+            for f, field in enumerate(levels):
+                for k, value in enumerate(field):
+                    for i in range(6):
+                        self.out[k, i, f : f + 1, :] = value[i : i + 1, :]
+            self.copies = []
+            for n, (o, deep, row, count) in enumerate(plan.blocks):
+                copy = pltpu.make_async_remote_copy(
+                    src_ref=self.out.at[pl.ds(0, deep), pl.ds(row, count)],
+                    dst_ref=self.box.at[plan.offsets.index(o), pl.ds(0, deep), pl.ds(row, count)],
+                    send_sem=ssem.at[n],
+                    recv_sem=rsem.at[n],
+                    device_id=peer(o),
+                    device_id_type=MESH,
+                )
+                copy.start()
+                self.copies.append(copy)
+
+        def wait(self):
+            for copy in self.copies:
+                copy.wait()
+
+        def row(self, o, k, i, f):
+            if dist(o) == 0:
+                return self.out[k - 1, i, f : f + 1, :]
+            return self.box[self.plan.offsets.index(o), k - 1, i, f : f + 1, :]
+
+        def faces(self, f):
+            return [self.row(moved_by((0, 0, 0), i), 1, i, f) for i in range(6)]
+
+        def arrived(self, v, k, f):
+            slot_ref = fresh("tile", tile_ref, 6)
             for i in range(6):
-                snd[k][i, f : f + 1, :] = field[i : i + 1, :]
-        copies = []
-        for p, (device, row, count) in enumerate(peers):
-            copy = pltpu.make_async_remote_copy(
-                src_ref=snd[k].at[pl.ds(row, count)],
-                dst_ref=rcv[k].at[pl.ds(row, count)],
-                send_sem=ssem.at[k, p],
-                recv_sem=rsem.at[k, p],
-                device_id=device,
-                device_id_type=MESH,
-            )
-            copy.start()
-            copies.append(copy)
-        return copies
-
-    def arrive(k, copies):
-        for copy in copies:
-            copy.wait()
-        return [[rcv[k][i, f : f + 1, :] for i in range(6)] for f in range(ROUND_FIELDS[k])]
+                slot_ref[i : i + 1, :] = self.row(moved_by(v, i), k, i, f)
+            return slot_ref[...]
+
+        def ghosts(self, f, depth, exits):
+            here = [(0, 0, 0)] + offsets(depth - 1)
+            values = {v: [self.arrived(v, k, f) for k in range(1, depth - dist(v) + 1)] for v in here}
+            for j in range(1, depth):
+                for v in here:
+                    if dist(v) > depth - j - 1:
+                        continue
+                    slot_ref = fresh("pile", pile_ref)
+                    for i in range(6):
+                        slot_ref[8 * i : 8 * i + 8, :] = values[moved_by(v, i)][j - 1]
+                    at = exits[v]
+                    for r in range(6):
+                        picked = jnp.take_along_axis(slot_ref[pl.ds(r, 8, stride=8), :], at.lo, axis=1)
+                        for k in range(j + 1, depth - dist(v) + 1):
+                            values[v][k - 1] = jnp.where(at.hi == 8 * (k - j) + r, picked, values[v][k - 1])
+            return values[(0, 0, 0)]
 
     def tile(n, ref, row):
         for j in range(8):
@@ -96,14 +202,15 @@
     slot = sub * 128 + lane
 
     list_ref[...] = jnp.full((8, 128), -1, I32)
-    list_ref[0:6, 0:W] = send_ref[...]
+    for b in range(6):
+        list_ref[LIST_ROW[b] : LIST_ROW[b] + 1, 0:W] = send_ref[b : b + 1, :]
     listed = list_ref[...]
     at_list = Index(listed)
     own = [tile(n, old_ref, n) for n in range(3)] + [tile(3 + n, new_ref, n) for n in range(3)] + [mass_ref[...]]
     own_rows = [rows_of(field) for field in own]
     fields = [at_list.look(field) for field in own_rows]
-    pl.semaphore_wait(barrier, 4)
-    moving = send(0, fields)
+    pl.semaphore_wait(barrier, len(offsets(DEEP)))
+    positions = Exchange(0, [[field] for field in fields])
 
     mass = own[6]
     rest = rest_ref[...]
@@ -122,6 +229,7 @@
         block = block + jnp.where(off >= W * t, 1, 0)
     remote = off >= 0
     lane_in = off - W * block
+    block = block + jnp.where(block >= 4, -2, jnp.where(block >= 2, 2, 0))
     ghost = 1024 + 128 * block + lane_in
     target = jnp.where(remote, 1024 + 128 * (block ^ 1) + 64 + lane_in, second)
     joins = jnp.logical_and(alive, first != second)
@@ -158,6 +266,8 @@
     left2, n2, sign2 = other(at_second, own2)
     n2 = jnp.where(remote, ghost, n2)
     at_n1, at_n2 = Index(n1), Index(n2)
+    turn1 = jnp.where(jnp.logical_and(n1 < 1024, sign1 > 0), n1 + 4096, n1)
+    turn2 = jnp.where(jnp.logical_and(n2 < 1024, sign2 > 0), n2 + 4096, n2)
     sign1 = jnp.where(n1 >= 1024, 1.0, sign1)
     sign2 = jnp.where(n2 >= 1024, 1.0, sign2)
 
@@ -165,10 +275,29 @@
     face_code = jnp.where(sub < 6, face_code, 0)
     face = (face_code & 4095) - 1
     face_sign = jnp.where(face_code >= 4096, 1.0, -1.0)
-    at_face = Index(face)
-
-    def at_faces(field):
-        return at_face.look(rows_of(field))
+    turn1_rows, turn2_rows = rows_of(turn1), rows_of(turn2)
+    at_level, ends = [], []
+    leaves = jnp.zeros((8, 128), I32)
+    current, came_first = face, face_code >= 4096
+    for k in range(1, DEEP + 1):
+        at = Index(current)
+        at_level.append(at)
+        ends.append(came_first)
+        follow = jnp.where(came_first, at.look(turn2_rows), at.look(turn1_rows))
+        follow = jnp.where(current >= 0, follow, -1)
+        outside = jnp.logical_and(follow >= 1024, follow < 4096)
+        leaves = jnp.where(outside, 1024 * k + follow - 1024, leaves)
+        current = jnp.where(jnp.logical_or(outside, follow < 0), -1, follow & 4095)
+        came_first = follow >= 4096
+    pointers = Exchange(1, [[leaves.astype(F32)]])
+
+    def at_faces(field, depth=1):
+        rows = rows_of(field)
+        return [at.look(rows) for at in at_level[:depth]]
+
+    def across(value):
+        value = pltpu.roll(value, 64, axis=1)
+        return jnp.where((sub & 1) == 0, pltpu.roll(value, 7, axis=0), pltpu.roll(value, 1, axis=0))
 
     from_first = [at_first.look(field) for field in own_rows]
     from_second = [at_second.look(field) for field in own_rows]
@@ -192,9 +321,9 @@
     headed = contract(jnp.concatenate(heads, 0), low)
     head_code = (headed[0:8] + 128.0 * headed[8:16]).astype(I32)
 
-    ghosts = arrive(0, moving)
+    positions.wait()
     at_ghost = Index(jnp.where(remote, ghost, -1))
-    from_second = [at_ghost.look(ghosts[f], 8, from_second[f]) for f in range(7)]
+    from_second = [at_ghost.look(positions.faces(f), 8, from_second[f]) for f in range(7)]
     span = [from_first[f] - from_second[f] for f in range(6)]
     mass1, mass2 = from_first[6], from_second[6]
     scale = jnp.where(alive, 1.0, 0.0) / jnp.sqrt(mass1 + mass2)
@@ -203,7 +332,7 @@
     arm = [scale * unit[n] for n in range(3)]
     pull = span[3:6]
     x = scale * (unit[0] * pull[0] + unit[1] * pull[1] + unit[2] * pull[2] - rest)
-    moving = send(1, [face_sign * at_faces(arm[n]) for n in range(3)] + [at_faces(x)])
+    arms = Exchange(2, [[face_sign * at_faces(arm[n])[0]] for n in range(3)] + [at_faces(x)])
 
     def dot3(a, b):
         return a[0] * b[0] + a[1] * b[1] + a[2] * b[2]
@@ -219,46 +348,82 @@
         return at_n1.look(rows), at_n2.look(rows)
 
     x1, x2 = near(x)
-    ghosts = arrive(1, moving)
-    via1 = [mass1 * at_n1.look(ghosts[n], 8, via1[n]) for n in range(3)]
-    via2 = [-mass2 * at_n2.look(ghosts[n], 8, via2[n]) for n in range(3)]
+    diag_levels = at_faces(diag, DEEP - 1)
+    pointers.wait()
+    exits = {v: Index(pointers.arrived(v, 1, 0).astype(I32)) for v in [(0, 0, 0)] + offsets(DEEP - 2)}
+
+    arms.wait()
+    arm_ghosts = [arms.faces(f) for f in range(4)]
+    via1 = [mass1 * at_n1.look(arm_ghosts[n], 8, via1[n]) for n in range(3)]
+    via2 = [-mass2 * at_n2.look(arm_ghosts[n], 8, via2[n]) for n in range(3)]
     e1 = -dot3(arm, via1)
     e2 = -dot3(arm, via2)
-    x1 = at_n1.look(ghosts[3], 8, x1)
-    x2 = at_n2.look(ghosts[3], 8, x2)
-
-    k = 2
-
-    def exchange(k, field):
-        moving = send(k, [at_faces(field)])
-        f1, f2 = near(field)
-        ghosts = arrive(k, moving)
-        return at_n1.look(ghosts[0], 8, f1), at_n2.look(ghosts[0], 8, f2), ghosts[0]
-
-    def expansion(k, x, x1, x2):
-        total = x
-        for step in range(ORDER):
+    x1 = at_n1.look(arm_ghosts[3], 8, x1)
+    x2 = at_n2.look(arm_ghosts[3], 8, x2)
+    total = x
+    x = diag * x + e1 * x1 + e2 * x2
+    total = total + x
+    first_number = 4
+    second_number = first_number + len(FIRST_PLAN)
+
+    e1_rows, e2_rows = rows_of(e1), rows_of(e2)
+    onward = [jnp.where(end, at.look(e2_rows), at.look(e1_rows)) for at, end in zip(at_level[: DEEP - 1], ends)]
+    inward = across(jnp.where(ends[0], at_level[0].look(e1_rows), at_level[0].look(e2_rows)))
+
+    def expansion(x, total, steps, depths, number, before=(), level1=None):
+        ghosts = []
+        diag_ghosts = link_ghosts = None
+        for step in range(steps + 1):
+            if not ghosts and (step < steps or level1 is not None):
+                depth = depths[0]
+                depths = depths[1:]
+                moving = Exchange(number, [at_faces(x, depth)])
+                number += 1
+                x1, x2 = near(x)
+                if diag_ghosts is None:
+                    tables, deep = before
+                    tables.wait()
+                    diag_ghosts = tables.ghosts(0, deep, exits)
+                    link_ghosts = [inward] + tables.ghosts(1, deep, exits)
+                moving.wait()
+                ghosts = moving.ghosts(0, depth, exits)
+            else:
+                x1, x2 = near(x)
+            if level1 is not None:
+                level1 = level1 + ghosts[0]
+            if step == steps:
+                break
+            rows = rows_of(ghosts[0], 6)
+            x1 = at_n1.look(rows, 8, x1)
+            x2 = at_n2.look(rows, 8, x2)
+            chain = [across(at_faces(x)[0]) if len(ghosts) > 1 else None] + ghosts
+            ghosts = [
+                diag_ghosts[k - 1] * chain[k] + link_ghosts[k - 1] * chain[k - 1] + link_ghosts[k] * chain[k + 1]
+                for k in range(1, len(chain) - 1)
+            ]
             x = diag * x + e1 * x1 + e2 * x2
             total = total + x
-            if step < ORDER - 1:
-                x1, x2, _ = exchange(k, x)
-                k += 1
-        return total, k
-
-    y, k = expansion(k, x, x1, x2)
-    y1, y2, _ = exchange(k, y)
-    k += 1
+        return total, level1
+
+    deep = max(FIRST_PLAN) - 1
+    tables = Exchange(3, [diag_levels[:deep], onward[:deep]])
+    y, _ = expansion(x, total, ORDER - 1, FIRST_PLAN, first_number, (tables, deep))
+    moving = Exchange(second_number + 1, [at_faces(y)])
+    deep = max(SECOND_PLAN) - 1
+    tables = Exchange(second_number, [diag_levels[:deep], onward[:deep]])
+    y1, y2 = near(y)
+    moving.wait()
+    y_ghost = moving.arrived((0, 0, 0), 1, 0)
+    rows = rows_of(y_ghost, 6)
+    y1 = at_n1.look(rows, 8, y1)
+    y2 = at_n2.look(rows, 8, y2)
     stretch = [pull[n] - (mass12 * arm[n] * y + via1[n] * y1 + via2[n] * y2) for n in range(3)]
     square = rest * rest
     goal = jnp.sqrt(jnp.maximum(2.0 * square - dot3(stretch, stretch), 0.25 * square))
     x = scale * (rest - goal)
-    x1, x2, _ = exchange(k, x)
-    k += 1
-    y_second, k = expansion(k, x, x1, x2)
-    z = y + y_second
+    z, z_ghost = expansion(x, y + x, ORDER, SECOND_PLAN, second_number + 2, (tables, deep), y_ghost)
     mult_ref[...] = z
 
-    moving = send(k, [at_faces(z)])
     z_rows = rows_of(z)
     has_head = head_code > 0
     head_first = head_code >= 4096
@@ -274,11 +439,10 @@
         head_first, at_head.look(rows_of(sign1)), at_head.look(rows_of(sign2))
     )
     arm_head = [turn * at_head.look(arm_rows[n]) for n in range(3)]
-    arm_tail = [at_tail.look(ghosts[n], 8, tail_sign * at_tail.look(arm_rows[n])) for n in range(3)]
+    arm_tail = [at_tail.look(arm_ghosts[n], 8, tail_sign * at_tail.look(arm_rows[n])) for n in range(3)]
     z_head = at_head.look(z_rows)
     z_tail = at_tail.look(z_rows)
-    last = arrive(k, moving)
-    z_tail = at_tail.look(last[0], 8, z_tail)
+    z_tail = at_tail.look(rows_of(z_ghost, 6), 8, z_tail)
     for n in range(3):
         moved = -mass * (arm_head[n] * z_head + arm_tail[n] * z_tail)
         for j in range(8):
@@ -287,17 +451,13 @@
 
 def per_device(old_pos, new_pos, inv_mass, rest_length, bond_pairs, live, send_index):
     vmem = pl.BlockSpec(memory_space=pltpu.VMEM)
-    rounds = len(ROUND_FIELDS)
-    faces = [pltpu.VMEM((6, f, 128), F32) for f in ROUND_FIELDS]
     disp, mult = pl.pallas_call(
         kernel,
         out_shape=(jax.ShapeDtypeStruct((3, 1024), F32), jax.ShapeDtypeStruct((8, 128), F32)),
         in_specs=[vmem] * 7,
         out_specs=(vmem, vmem),
-        scratch_shapes=[pltpu.VMEM((6, 8, 128), F32), pltpu.VMEM((8, 128), I32)]
-        + faces
-        + faces
-        + [pltpu.SemaphoreType.DMA((rounds, 4)), pltpu.SemaphoreType.DMA((rounds, 4))],
+        scratch_shapes=[pltpu.VMEM((512, 8, 128), F32), pltpu.VMEM((8, 128), I32), pltpu.VMEM((192, 64, 128), F32)]
+        + [shape for plan in plans() for shape in plan.shapes()],
         compiler_params=pltpu.CompilerParams(collective_id=0, has_side_effects=True),
         name="plincs",
     )(

time: 74.3 us -> 49.2 us (0.66)
  Pallas kernels: 71.5 us -> 46.5 us
    pallas_call x1, Pallas kernels: 71.5 us -> 46.5 us  [per_device(): pl.pallas_call(kernel, out_shape=(jax.ShapeDtypeStruct((3, 1024), F32), j...]
where the time goes in v1:
time: 49.2 us; the launch traced here: 49 us
  Pallas kernels  46.5 us (95%)
  local copies, waits for them, and re-layouts  1.92 us (4%)
  between operations  0.65 us (1%)
    pallas_call x1, Pallas kernels, per_device(): pl.pallas_call(kernel, out_shape=(jax.ShapeDtypeStruct((3, 1024), F32), j...  46.5 us
    unnamed x4, local copies, waits for them, and re-layouts  1.92 us

profile of v1, /device:TPU:1, one launch (start us, length us, event | category | flops | bytes accessed | tf_op | source)
XLA Modules:
  0.0 49.0 jit_solution(13924099313005104738)
XLA Ops:
  0.6 46.5 %plincs.1 = (f32[3,1024]{1,0:T(4,128)}, f32[8,128]{1,0:T(8,128)}) custom-call(f32[3,1024]{1,0:T(4,128)} %old_ref.1, f32[3,1024]{1,0:T(4,128)} %new_ref.1, f32[8,128]{1,0:T(8,128)} %bitcast.4, f32[8,128]{1,0:T(8,128)} %bitcast.5, s32[2,1024]{1,0:T(2,128)} %pair_ref.1, s32[8,128]{1,0:T(8,128)} %bitcast.6, s32[6,48]{1,0:T(8,128)} %send_ref.1), custom_call_target="tpu_custom_call" | custom-call | tf_op jit(solution)/shard_map/plincs/pallas_call | solution.py:454
  47.1 0.0 copy-start
  47.1 1.3 %copy.11 = f32[3,1024]{1,0:T(4,128)} copy(f32[3,1024]{1,0:T(4,128)} %get-tuple-element.8) | data formatting | bytes 24576
  48.4 0.0 copy-done
  48.4 0.6 %copy.12 = f32[1024]{0:T(1024)} copy(f32[1024]{0:T(1024)S(1)} %bitcast.7) | data formatting | bytes 8192
Async XLA Ops:
  47.1 1.3 %copy-start = (f32[8,128]{1,0:T(8,128)S(1)}, f32[8,128]{1,0:T(8,128)}, u32[]{:S(2)}) copy-start(f32[8,128]{1,0:T(8,128)} %get-tuple-element.5) | copy-start | bytes 12292

commit v2 on v1

--- a/solution.py
+++ b/solution.py
@@ -10,9 +10,8 @@
 W = 48
 F32 = jnp.float32
 I32 = jnp.int32
-FIRST_PLAN = (3,)
-SECOND_PLAN = (5,)
-DEEP = max(FIRST_PLAN + SECOND_PLAN)
+GIVEN = (((3, 1024), F32), ((3, 1024), F32), ((8, 128), F32), ((8, 128), F32), ((2, 1024), I32), ((8, 128), I32), ((6, W), I32))
+FIRST, SECOND = 4, 5
 LIST_ROW = (0, 1, 4, 5, 2, 3)
 STEPS = ((1, 0, 0), (1, 0, 0), (0, 0, -1), (0, 0, 1), (0, 1, 0), (0, 1, 0))
 
@@ -66,11 +65,7 @@
 
 
 def plans():
-    out = [Plan(1, 7), Plan(DEEP - 1, 1, 1), Plan(1, 4), Plan(max(FIRST_PLAN) - 1, 2)]
-    out += [Plan(d, 1) for d in FIRST_PLAN]
-    out += [Plan(max(SECOND_PLAN) - 1, 2), Plan(1, 1)]
-    out += [Plan(d, 1) for d in SECOND_PLAN]
-    return out
+    return [Plan(1, 7), Plan(SECOND - 1, 1, 1), Plan(1, 4), Plan(FIRST - 1, 2), Plan(FIRST, 1), Plan(1, 2), Plan(SECOND, 1)]
 
 
 def lane_pick(row, lo):
@@ -109,7 +104,9 @@
     return lax.dot_general(a, b, (((1,), (1,)), ((), ())), preferred_element_type=F32)
 
 
-def kernel(old_ref, new_ref, mass_ref, rest_ref, pair_ref, live_ref, send_ref, disp_ref, mult_ref, tile_ref, list_ref, pile_ref, *bufs):
+def kernel(*refs):
+    given, (disp_ref, mult_ref, tile_ref, list_ref, pile_ref), bufs = refs[:7], refs[7:12], refs[12:]
+    taken, take_sem, bufs = bufs[:7], bufs[7], bufs[8:]
     ix, iy, iz = lax.axis_index("gx"), lax.axis_index("gy"), lax.axis_index("gz")
     nz = lax.axis_size("gz")
 
@@ -124,8 +121,13 @@
         return device
 
     barrier = pltpu.get_barrier_semaphore()
-    for o in offsets(DEEP):
+    for o in offsets(SECOND):
         pl.semaphore_signal(barrier, inc=1, device_id=peer(o), device_id_type=MESH)
+
+    takes = [pltpu.make_async_copy(given[n], taken[n], take_sem.at[n]) for n in range(7)]
+    for n in (6, 0, 1, 2, 4, 5, 3):
+        takes[n].start()
+    old_ref, new_ref, mass_ref, rest_ref, pair_ref, live_ref, send_ref = taken
 
     todo = plans()
 
@@ -201,6 +203,8 @@
     sub = lax.broadcasted_iota(I32, (8, 128), 0)
     slot = sub * 128 + lane
 
+    for take in takes:
+        take.wait()
     list_ref[...] = jnp.full((8, 128), -1, I32)
     for b in range(6):
         list_ref[LIST_ROW[b] : LIST_ROW[b] + 1, 0:W] = send_ref[b : b + 1, :]
@@ -209,7 +213,7 @@
     own = [tile(n, old_ref, n) for n in range(3)] + [tile(3 + n, new_ref, n) for n in range(3)] + [mass_ref[...]]
     own_rows = [rows_of(field) for field in own]
     fields = [at_list.look(field) for field in own_rows]
-    pl.semaphore_wait(barrier, len(offsets(DEEP)))
+    pl.semaphore_wait(barrier, len(offsets(SECOND)))
     positions = Exchange(0, [[field] for field in fields])
 
     mass = own[6]
@@ -279,7 +283,7 @@
     at_level, ends = [], []
     leaves = jnp.zeros((8, 128), I32)
     current, came_first = face, face_code >= 4096
-    for k in range(1, DEEP + 1):
+    for k in range(1, SECOND + 1):
         at = Index(current)
         at_level.append(at)
         ends.append(came_first)
@@ -348,9 +352,9 @@
         return at_n1.look(rows), at_n2.look(rows)
 
     x1, x2 = near(x)
-    diag_levels = at_faces(diag, DEEP - 1)
+    diag_levels = at_faces(diag, SECOND - 1)
     pointers.wait()
-    exits = {v: Index(pointers.arrived(v, 1, 0).astype(I32)) for v in [(0, 0, 0)] + offsets(DEEP - 2)}
+    exits = {v: Index(pointers.arrived(v, 1, 0).astype(I32)) for v in [(0, 0, 0)] + offsets(SECOND - 2)}
 
     arms.wait()
     arm_ghosts = [arms.faces(f) for f in range(4)]
@@ -360,60 +364,41 @@
     e2 = -dot3(arm, via2)
     x1 = at_n1.look(arm_ghosts[3], 8, x1)
     x2 = at_n2.look(arm_ghosts[3], 8, x2)
-    total = x
-    x = diag * x + e1 * x1 + e2 * x2
-    total = total + x
-    first_number = 4
-    second_number = first_number + len(FIRST_PLAN)
-
     e1_rows, e2_rows = rows_of(e1), rows_of(e2)
-    onward = [jnp.where(end, at.look(e2_rows), at.look(e1_rows)) for at, end in zip(at_level[: DEEP - 1], ends)]
+    onward = [jnp.where(end, at.look(e2_rows), at.look(e1_rows)) for at, end in zip(at_level[: SECOND - 1], ends)]
     inward = across(jnp.where(ends[0], at_level[0].look(e1_rows), at_level[0].look(e2_rows)))
 
-    def expansion(x, total, steps, depths, number, before=(), level1=None):
-        ghosts = []
-        diag_ghosts = link_ghosts = None
-        for step in range(steps + 1):
-            if not ghosts and (step < steps or level1 is not None):
-                depth = depths[0]
-                depths = depths[1:]
-                moving = Exchange(number, [at_faces(x, depth)])
-                number += 1
-                x1, x2 = near(x)
-                if diag_ghosts is None:
-                    tables, deep = before
-                    tables.wait()
-                    diag_ghosts = tables.ghosts(0, deep, exits)
-                    link_ghosts = [inward] + tables.ghosts(1, deep, exits)
-                moving.wait()
-                ghosts = moving.ghosts(0, depth, exits)
-            else:
-                x1, x2 = near(x)
-            if level1 is not None:
-                level1 = level1 + ghosts[0]
-            if step == steps:
-                break
-            rows = rows_of(ghosts[0], 6)
-            x1 = at_n1.look(rows, 8, x1)
-            x2 = at_n2.look(rows, 8, x2)
-            chain = [across(at_faces(x)[0]) if len(ghosts) > 1 else None] + ghosts
-            ghosts = [
-                diag_ghosts[k - 1] * chain[k] + link_ghosts[k - 1] * chain[k - 1] + link_ghosts[k] * chain[k + 1]
-                for k in range(1, len(chain) - 1)
-            ]
-            x = diag * x + e1 * x1 + e2 * x2
-            total = total + x
-        return total, level1
-
-    deep = max(FIRST_PLAN) - 1
-    tables = Exchange(3, [diag_levels[:deep], onward[:deep]])
-    y, _ = expansion(x, total, ORDER - 1, FIRST_PLAN, first_number, (tables, deep))
-    moving = Exchange(second_number + 1, [at_faces(y)])
-    deep = max(SECOND_PLAN) - 1
-    tables = Exchange(second_number, [diag_levels[:deep], onward[:deep]])
+    def step(x, x1, x2, ghosts, diag_ghosts, link_ghosts):
+        rows = rows_of(ghosts[0], 6)
+        x1 = at_n1.look(rows, 8, x1)
+        x2 = at_n2.look(rows, 8, x2)
+        chain = [across(at_faces(x)[0]) if len(ghosts) > 1 else None] + ghosts
+        ghosts = [
+            diag_ghosts[k - 1] * chain[k] + link_ghosts[k - 1] * chain[k - 1] + link_ghosts[k] * chain[k + 1]
+            for k in range(1, len(chain) - 1)
+        ]
+        return diag * x + e1 * x1 + e2 * x2, ghosts
+
+    y = x
+    y_ghost = jnp.concatenate(arm_ghosts[3] + arm_ghosts[3][:2], 0)
+    x, _ = step(x, x1, x2, [y_ghost], None, None)
+    moving = Exchange(4, [at_faces(x, FIRST)])
+    tables = Exchange(3, [diag_levels[: FIRST - 1], onward[: FIRST - 1]])
+    x1, x2 = near(x)
+    tables.wait()
+    diag_ghosts = tables.ghosts(0, FIRST - 1, exits)
+    link_ghosts = [inward] + tables.ghosts(1, FIRST - 1, exits)
+    moving.wait()
+    ghosts = moving.ghosts(0, FIRST, exits)
+    for n in range(ORDER):
+        y = y + x
+        y_ghost = y_ghost + ghosts[0]
+        if n == ORDER - 1:
+            break
+        x, ghosts = step(x, x1, x2, ghosts, diag_ghosts, link_ghosts)
+        x1, x2 = near(x)
+
     y1, y2 = near(y)
-    moving.wait()
-    y_ghost = moving.arrived((0, 0, 0), 1, 0)
     rows = rows_of(y_ghost, 6)
     y1 = at_n1.look(rows, 8, y1)
     y2 = at_n2.look(rows, 8, y2)
@@ -421,7 +406,30 @@
     square = rest * rest
     goal = jnp.sqrt(jnp.maximum(2.0 * square - dot3(stretch, stretch), 0.25 * square))
     x = scale * (rest - goal)
-    z, z_ghost = expansion(x, y + x, ORDER, SECOND_PLAN, second_number + 2, (tables, deep), y_ghost)
+    moving = Exchange(6, [at_faces(x, SECOND)])
+
+    at_exit = Index(leaves)
+
+    def resolved(value, ghost_levels):
+        for t in range(1, SECOND - 1):
+            value = at_exit.look(rows_of(ghost_levels[SECOND - 2 - t], 6), 8 * t, value)
+        return value
+
+    last = Exchange(5, [[resolved(diag_levels[-1], diag_ghosts)], [resolved(onward[-1], link_ghosts[1:])]])
+    x1, x2 = near(x)
+    last.wait()
+    diag_ghosts = diag_ghosts + [last.arrived((0, 0, 0), 1, 0)]
+    link_ghosts = link_ghosts + [last.arrived((0, 0, 0), 1, 1)]
+    moving.wait()
+    ghosts = moving.ghosts(0, SECOND, exits)
+    z, z_ghost = y, y_ghost
+    for n in range(ORDER + 1):
+        z = z + x
+        z_ghost = z_ghost + ghosts[0]
+        if n == ORDER:
+            break
+        x, ghosts = step(x, x1, x2, ghosts, diag_ghosts, link_ghosts)
+        x1, x2 = near(x)
     mult_ref[...] = z
 
     z_rows = rows_of(z)
@@ -454,9 +462,11 @@
     disp, mult = pl.pallas_call(
         kernel,
         out_shape=(jax.ShapeDtypeStruct((3, 1024), F32), jax.ShapeDtypeStruct((8, 128), F32)),
-        in_specs=[vmem] * 7,
+        in_specs=[pl.BlockSpec(memory_space=pl.ANY)] * 7,
         out_specs=(vmem, vmem),
         scratch_shapes=[pltpu.VMEM((512, 8, 128), F32), pltpu.VMEM((8, 128), I32), pltpu.VMEM((192, 64, 128), F32)]
+        + [pltpu.VMEM(shape, kind) for shape, kind in GIVEN]
+        + [pltpu.SemaphoreType.DMA((7,))]
         + [shape for plan in plans() for shape in plan.shapes()],
         compiler_params=pltpu.CompilerParams(collective_id=0, has_side_effects=True),
         name="plincs",

time: 49.2 us -> 46.2 us (0.939)
  Pallas kernels: 46.5 us -> 43.5 us
    pallas_call x1, Pallas kernels: 46.5 us -> 43.5 us  [per_device(): pl.pallas_call(kernel, out_shape=(jax.ShapeDtypeStruct((3, 1024), F32), j...]
where the time goes in v2:
time: 46.2 us; the launch traced here: 46 us
  Pallas kernels  43.5 us (94%)
  local copies, waits for them, and re-layouts  1.92 us (4%)
  between operations  0.65 us (1%)
    pallas_call x1, Pallas kernels, per_device(): pl.pallas_call(kernel, out_shape=(jax.ShapeDtypeStruct((3, 1024), F32), j...  43.5 us
    unnamed x4, local copies, waits for them, and re-layouts  1.92 us

profile of v2, /device:TPU:1, one launch (start us, length us, event | category | flops | bytes accessed | tf_op | source)
XLA Modules:
  0.0 46.0 jit_solution(15016615218974550952)
XLA Ops:
  0.6 43.5 %plincs.1 = (f32[3,1024]{1,0:T(4,128)}, f32[8,128]{1,0:T(8,128)}) custom-call(f32[3,1024]{1,0:T(4,128)} %refs_0_.1, f32[3,1024]{1,0:T(4,128)} %refs_1_.1, f32[8,128]{1,0:T(8,128)} %bitcast.4, f32[8,128]{1,0:T(8,128)} %bitcast.5, s32[2,1024]{1,0:T(2,128)} %refs_4_.1, s32[8,128]{1,0:T(8,128)} %bitcast.6, s32[6,48]{1,0:T(8,128)} %refs_6_.1), custom_call_target="tpu_custom_call" | custom-call | tf_op jit(solution)/shard_map/plincs/pallas_call | solution.py:462
  44.1 0.0 copy-start
  44.1 1.3 %copy.11 = f32[3,1024]{1,0:T(4,128)} copy(f32[3,1024]{1,0:T(4,128)} %get-tuple-element.8) | data formatting | bytes 24576
  45.4 0.0 copy-done
  45.4 0.6 %copy.12 = f32[1024]{0:T(1024)} copy(f32[1024]{0:T(1024)S(1)} %bitcast.7) | data formatting | bytes 8192
Async XLA Ops:
  44.1 1.3 %copy-start = (f32[8,128]{1,0:T(8,128)S(1)}, f32[8,128]{1,0:T(8,128)}, u32[]{:S(2)}) copy-start(f32[8,128]{1,0:T(8,128)} %get-tuple-element.5) | copy-start | bytes 12292

commit v3 on v2

--- a/solution.py
+++ b/solution.py
@@ -36,14 +36,9 @@
         need = [max(0, depth - dist(moved_by(o, i, -1))) for i in range(6)]
         if levels is not None:
             need = [min(n, levels) for n in need]
-        i = 0
-        while i < 6:
-            j = i
-            while j < 6 and need[j] == need[i]:
-                j += 1
-            if need[i]:
-                out.append((o, need[i], i, j - i))
-            i = j
+        hit = [i for i in range(6) if need[i]]
+        if hit:
+            out.append((o, max(need), hit[0], hit[-1] - hit[0] + 1))
     return out
 
 
@@ -65,7 +60,7 @@
 
 
 def plans():
-    return [Plan(1, 7), Plan(SECOND - 1, 1, 1), Plan(1, 4), Plan(FIRST - 1, 2), Plan(FIRST, 1), Plan(1, 2), Plan(SECOND, 1)]
+    return [Plan(2, 4, 1), Plan(1, 9), Plan(SECOND - 1, 1, 1), Plan(FIRST - 1, 2), Plan(FIRST, 1), Plan(1, 2), Plan(SECOND, 1)]
 
 
 def lane_pick(row, lo):
@@ -213,8 +208,6 @@
     own = [tile(n, old_ref, n) for n in range(3)] + [tile(3 + n, new_ref, n) for n in range(3)] + [mass_ref[...]]
     own_rows = [rows_of(field) for field in own]
     fields = [at_list.look(field) for field in own_rows]
-    pl.semaphore_wait(barrier, len(offsets(SECOND)))
-    positions = Exchange(0, [[field] for field in fields])
 
     mass = own[6]
     rest = rest_ref[...]
@@ -278,7 +271,6 @@
     face_code = jnp.where(lane < 64, at_list.look(code_rows), code[8:16])
     face_code = jnp.where(sub < 6, face_code, 0)
     face = (face_code & 4095) - 1
-    face_sign = jnp.where(face_code >= 4096, 1.0, -1.0)
     turn1_rows, turn2_rows = rows_of(turn1), rows_of(turn2)
     at_level, ends = [], []
     leaves = jnp.zeros((8, 128), I32)
@@ -293,7 +285,15 @@
         leaves = jnp.where(outside, 1024 * k + follow - 1024, leaves)
         current = jnp.where(jnp.logical_or(outside, follow < 0), -1, follow & 4095)
         came_first = follow >= 4096
-    pointers = Exchange(1, [[leaves.astype(F32)]])
+    packed = [jnp.where(lane < 64, fields[f], pltpu.roll(fields[f + 4], 64, axis=1)) for f in range(3)] + [fields[3]]
+    face_rest = at_level[0].look(rows_of(rest))
+    far_atom = jnp.where(ends[0], at_level[0].look(rows_of(second)), at_level[0].look(rows_of(first)))
+    at_far = Index(jnp.where(face_rest > 0, far_atom, -1))
+    far_fields = [at_far.look(field) for field in own_rows] + [face_rest, leaves.astype(F32)]
+    pl.semaphore_wait(barrier, len(offsets(SECOND)))
+    nears = Exchange(0, [[field] for field in packed])
+    fars = Exchange(1, [[field] for field in far_fields])
+    pointers = Exchange(2, [[leaves.astype(F32)]])
 
     def at_faces(field, depth=1):
         rows = rows_of(field)
@@ -325,9 +325,9 @@
     headed = contract(jnp.concatenate(heads, 0), low)
     head_code = (headed[0:8] + 128.0 * headed[8:16]).astype(I32)
 
-    positions.wait()
-    at_ghost = Index(jnp.where(remote, ghost, -1))
-    from_second = [at_ghost.look(positions.faces(f), 8, from_second[f]) for f in range(7)]
+    nears.wait()
+    at_ghost = [Index(jnp.where(remote, ghost + half, -1)) for half in (0, 64)]
+    from_second = [at_ghost[f // 4].look(nears.faces(f % 4), 8, from_second[f]) for f in range(7)]
     span = [from_first[f] - from_second[f] for f in range(6)]
     mass1, mass2 = from_first[6], from_second[6]
     scale = jnp.where(alive, 1.0, 0.0) / jnp.sqrt(mass1 + mass2)
@@ -336,7 +336,6 @@
     arm = [scale * unit[n] for n in range(3)]
     pull = span[3:6]
     x = scale * (unit[0] * pull[0] + unit[1] * pull[1] + unit[2] * pull[2] - rest)
-    arms = Exchange(2, [[face_sign * at_faces(arm[n])[0]] for n in range(3)] + [at_faces(x)])
 
     def dot3(a, b):
         return a[0] * b[0] + a[1] * b[1] + a[2] * b[2]
@@ -353,11 +352,35 @@
 
     x1, x2 = near(x)
     diag_levels = at_faces(diag, SECOND - 1)
-    pointers.wait()
-    exits = {v: Index(pointers.arrived(v, 1, 0).astype(I32)) for v in [(0, 0, 0)] + offsets(SECOND - 2)}
-
-    arms.wait()
-    arm_ghosts = [arms.faces(f) for f in range(4)]
+
+    here = (0, 0, 0)
+    arrived = [nears.arrived(here, 1, f) for f in range(4)]
+    near_atom = [
+        jnp.where(lane < 64, arrived[f] if f < 4 else pltpu.roll(arrived[f - 4], 64, axis=1), across(fields[f])) for f in range(7)
+    ]
+    fars.wait()
+    far_atom = [fars.arrived(here, 1, f) for f in range(8)]
+    leave = fars.arrived(here, 1, 8).astype(I32)
+    leave_lane = leave & 127
+    leave_row = jnp.where(leave_lane < 64, leave >> 7, -1)
+    seen = {v: [nears.arrived(v, 1, f) for f in range(4)] for v in offsets(1)}
+    for f in range(4):
+        slot_ref = fresh("pile", pile_ref)
+        for i in range(6):
+            slot_ref[8 * i : 8 * i + 8, :] = seen[moved_by(here, i)][f]
+        for r in range(6):
+            table = slot_ref[pl.ds(r, 8, stride=8), :]
+            for half in range(2):
+                if f + 4 * half < 7:
+                    picked = jnp.take_along_axis(table, (leave_lane + 64 * half) & 127, axis=1)
+                    far_atom[f + 4 * half] = jnp.where(leave_row == 8 + r, picked, far_atom[f + 4 * half])
+    ghost_rest = far_atom[7]
+    there = ghost_rest > 0
+    ghost_span = [near_atom[f] - far_atom[f] for f in range(6)]
+    ghost_scale = jnp.where(there, 1.0, 0.0) / jnp.sqrt(jnp.where(there, near_atom[6] + far_atom[6], 1.0))
+    ghost_unit = [ghost_span[n] / jnp.sqrt(dot3(ghost_span[:3], ghost_span[:3]) + 0.25) for n in range(3)]
+    x_ghost = ghost_scale * (dot3(ghost_unit, ghost_span[3:]) - ghost_rest)
+    arm_ghosts = [rows_of(ghost_scale * ghost_unit[n], 6) for n in range(3)] + [rows_of(x_ghost, 6)]
     via1 = [mass1 * at_n1.look(arm_ghosts[n], 8, via1[n]) for n in range(3)]
     via2 = [-mass2 * at_n2.look(arm_ghosts[n], 8, via2[n]) for n in range(3)]
     e1 = -dot3(arm, via1)
@@ -380,11 +403,13 @@
         return diag * x + e1 * x1 + e2 * x2, ghosts
 
     y = x
-    y_ghost = jnp.concatenate(arm_ghosts[3] + arm_ghosts[3][:2], 0)
+    y_ghost = x_ghost
     x, _ = step(x, x1, x2, [y_ghost], None, None)
     moving = Exchange(4, [at_faces(x, FIRST)])
     tables = Exchange(3, [diag_levels[: FIRST - 1], onward[: FIRST - 1]])
     x1, x2 = near(x)
+    pointers.wait()
+    exits = {v: Index(pointers.arrived(v, 1, 0).astype(I32)) for v in [(0, 0, 0)] + offsets(SECOND - 2)}
     tables.wait()
     diag_ghosts = tables.ghosts(0, FIRST - 1, exits)
     link_ghosts = [inward] + tables.ghosts(1, FIRST - 1, exits)

time: 46.2 us -> 39.4 us (0.85)
  Pallas kernels: 43.5 us -> 36.6 us
    pallas_call x1, Pallas kernels: 43.5 us -> 36.6 us  [per_device(): pl.pallas_call(kernel, out_shape=(jax.ShapeDtypeStruct((3, 1024), F32), j...]
where the time goes in v3:
time: 39.4 us; the launch traced here: 39.2 us
  Pallas kernels  36.6 us (93%)
  local copies, waits for them, and re-layouts  1.92 us (5%)
  between operations  0.65 us (2%)
    pallas_call x1, Pallas kernels, per_device(): pl.pallas_call(kernel, out_shape=(jax.ShapeDtypeStruct((3, 1024), F32), j...  36.6 us
    unnamed x4, local copies, waits for them, and re-layouts  1.92 us

profile of v3, /device:TPU:1, one launch (start us, length us, event | category | flops | bytes accessed | tf_op | source)
XLA Modules:
  0.0 39.2 jit_solution(468340620313712969)
XLA Ops:
  0.6 36.6 %plincs.1 = (f32[3,1024]{1,0:T(4,128)}, f32[8,128]{1,0:T(8,128)}) custom-call(f32[3,1024]{1,0:T(4,128)} %refs_0_.1, f32[3,1024]{1,0:T(4,128)} %refs_1_.1, f32[8,128]{1,0:T(8,128)} %bitcast.4, f32[8,128]{1,0:T(8,128)} %bitcast.5, s32[2,1024]{1,0:T(2,128)} %refs_4_.1, s32[8,128]{1,0:T(8,128)} %bitcast.6, s32[6,48]{1,0:T(8,128)} %refs_6_.1), custom_call_target="tpu_custom_call" | custom-call | tf_op jit(solution)/shard_map/plincs/pallas_call | solution.py:487
  37.3 0.0 copy-start
  37.3 1.3 %copy.11 = f32[3,1024]{1,0:T(4,128)} copy(f32[3,1024]{1,0:T(4,128)} %get-tuple-element.8) | data formatting | bytes 24576
  38.6 0.0 copy-done
  38.6 0.6 %copy.12 = f32[1024]{0:T(1024)} copy(f32[1024]{0:T(1024)S(1)} %bitcast.7) | data formatting | bytes 8192
Async XLA Ops:
  37.3 1.3 %copy-start = (f32[8,128]{1,0:T(8,128)S(1)}, f32[8,128]{1,0:T(8,128)}, u32[]{:S(2)}) copy-start(f32[8,128]{1,0:T(8,128)} %get-tuple-element.5) | copy-start | bytes 12292

commit v4 on v3

--- a/solution.py
+++ b/solution.py
@@ -37,8 +37,16 @@
         if levels is not None:
             need = [min(n, levels) for n in need]
         hit = [i for i in range(6) if need[i]]
+        runs = []
+        for i in hit:
+            if runs and runs[-1][2] + runs[-1][3] == i and runs[-1][1] == need[i]:
+                runs[-1] = (o, need[i], runs[-1][2], runs[-1][3] + 1)
+            else:
+                runs.append((o, need[i], i, 1))
         if hit:
-            out.append((o, max(need), hit[0], hit[-1] - hit[0] + 1))
+            whole = (o, max(need), hit[0], hit[-1] - hit[0] + 1)
+            spare = whole[1] * whole[3] - sum(need)
+            out += runs if len(runs) > 1 and spare >= (4 if len(runs) == 2 else 10) else [whole]
     return out
 
 
@@ -423,6 +431,14 @@
         x, ghosts = step(x, x1, x2, ghosts, diag_ghosts, link_ghosts)
         x1, x2 = near(x)
 
+    at_exit = Index(leaves)
+
+    def resolved(value, ghost_levels):
+        for t in range(1, SECOND - 1):
+            value = at_exit.look(rows_of(ghost_levels[SECOND - 2 - t], 6), 8 * t, value)
+        return value
+
+    last = Exchange(5, [[resolved(diag_levels[-1], diag_ghosts)], [resolved(onward[-1], link_ghosts[1:])]])
     y1, y2 = near(y)
     rows = rows_of(y_ghost, 6)
     y1 = at_n1.look(rows, 8, y1)
@@ -433,14 +449,6 @@
     x = scale * (rest - goal)
     moving = Exchange(6, [at_faces(x, SECOND)])
 
-    at_exit = Index(leaves)
-
-    def resolved(value, ghost_levels):
-        for t in range(1, SECOND - 1):
-            value = at_exit.look(rows_of(ghost_levels[SECOND - 2 - t], 6), 8 * t, value)
-        return value
-
-    last = Exchange(5, [[resolved(diag_levels[-1], diag_ghosts)], [resolved(onward[-1], link_ghosts[1:])]])
     x1, x2 = near(x)
     last.wait()
     diag_ghosts = diag_ghosts + [last.arrived((0, 0, 0), 1, 0)]
@@ -486,7 +494,7 @@
     vmem = pl.BlockSpec(memory_space=pltpu.VMEM)
     disp, mult = pl.pallas_call(
         kernel,
-        out_shape=(jax.ShapeDtypeStruct((3, 1024), F32), jax.ShapeDtypeStruct((8, 128), F32)),
+        out_shape=(pltpu.VMEM((3, 1024), F32), pltpu.VMEM((8, 128), F32)),
         in_specs=[pl.BlockSpec(memory_space=pl.ANY)] * 7,
         out_specs=(vmem, vmem),
         scratch_shapes=[pltpu.VMEM((512, 8, 128), F32), pltpu.VMEM((8, 128), I32), pltpu.VMEM((192, 64, 128), F32)]

time: 39.4 us -> 37.3 us (0.947)
  Pallas kernels: 36.6 us -> 35.4 us
  local copies, waits for them, and re-layouts: 1.92 us -> 1.2 us
    pallas_call x1, Pallas kernels: 36.6 us -> 35.4 us  [per_device(): pl.pallas_call(kernel, out_shape=(pltpu.VMEM((3, 1024), F32), pltpu.VMEM(...]
    unnamed x4 -> x2, local copies, waits for them, and re-layouts: 1.92 us -> 1.2 us
where the time goes in v4:
time: 37.3 us; the launch traced here: 37.2 us
  Pallas kernels  35.4 us (95%)
  local copies, waits for them, and re-layouts  1.2 us (3%)
  between operations  0.64 us (2%)
    pallas_call x1, Pallas kernels, per_device(): pl.pallas_call(kernel, out_shape=(pltpu.VMEM((3, 1024), F32), pltpu.VMEM(...  35.4 us
    unnamed x2, local copies, waits for them, and re-layouts  1.2 us

profile of v4, /device:TPU:1, one launch (start us, length us, event | category | flops | bytes accessed | tf_op | source)
XLA Modules:
  0.0 37.2 jit_solution(4664920076319770413)
XLA Ops:
  0.6 35.4 %plincs.1 = (f32[3,1024]{1,0:T(4,128)S(1)}, f32[8,128]{1,0:T(8,128)S(1)}) custom-call(f32[3,1024]{1,0:T(4,128)} %refs_0_.1, f32[3,1024]{1,0:T(4,128)} %refs_1_.1, f32[8,128]{1,0:T(8,128)} %bitcast.5, f32[8,128]{1,0:T(8,128)} %bitcast.6, s32[2,1024]{1,0:T(2,128)} %refs_4_.1, s32[8,128]{1,0:T(8,128)} %bitcast.7, s32[6,48]{1,0:T(8,128)} %refs_6_.1), custom_call_target="tpu_custom_call" | custom-call | tf_op jit(solution)/shard_map/plincs/pallas_call | solution.py:495
  36.0 0.6 %copy.11 = f32[3,1024]{1,0:T(4,128)} copy(f32[3,1024]{1,0:T(4,128)S(1)} %get-tuple-element.6) | data formatting | bytes 24576
  36.6 0.6 %copy.12 = f32[1024]{0:T(1024)} copy(f32[1024]{0:T(1024)S(1)} %bitcast.4) | data formatting | bytes 8192

commit v5 on v4

--- a/solution.py
+++ b/solution.py
@@ -30,45 +30,32 @@
     return [o for o in every if 0 < dist(o) <= depth]
 
 
-def blocks(depth, levels=None):
-    out = []
-    for o in offsets(depth):
-        need = [max(0, depth - dist(moved_by(o, i, -1))) for i in range(6)]
-        if levels is not None:
-            need = [min(n, levels) for n in need]
-        hit = [i for i in range(6) if need[i]]
-        runs = []
-        for i in hit:
-            if runs and runs[-1][2] + runs[-1][3] == i and runs[-1][1] == need[i]:
-                runs[-1] = (o, need[i], runs[-1][2], runs[-1][3] + 1)
-            else:
-                runs.append((o, need[i], i, 1))
-        if hit:
-            whole = (o, max(need), hit[0], hit[-1] - hit[0] + 1)
-            spare = whole[1] * whole[3] - sum(need)
-            out += runs if len(runs) > 1 and spare >= (4 if len(runs) == 2 else 10) else [whole]
-    return out
-
-
 class Plan:
-    def __init__(self, depth, fields, levels=None):
-        self.depth, self.fields = depth, fields
-        self.levels = depth if levels is None else levels
-        self.blocks = blocks(depth, levels)
-        self.offsets = offsets(depth)
+    def __init__(self, *fields):
+        self.messages, self.place, self.rows = [], {}, 0
+        for o in offsets(max(depth for depth, _ in fields)):
+            start = self.rows
+            for f, (depth, levels) in enumerate(fields):
+                for i in range(6):
+                    for k in range(1, min(levels, depth - dist(moved_by(o, i, -1))) + 1):
+                        self.place[o, k, i, f] = self.rows
+                        self.rows += 1
+            self.messages.append((o, start, self.rows - start))
 
     def shapes(self):
-        box = (self.levels, 6, self.fields, 128)
-        return [
-            pltpu.VMEM(box, F32),
-            pltpu.VMEM((len(self.offsets),) + box, F32),
-            pltpu.SemaphoreType.DMA((len(self.blocks),)),
-            pltpu.SemaphoreType.DMA((len(self.blocks),)),
-        ]
+        rows = pltpu.VMEM((self.rows, 1, 128), F32)
+        sems = pltpu.SemaphoreType.DMA((len(self.messages),))
+        return [rows, rows, sems, sems]
 
 
 def plans():
-    return [Plan(2, 4, 1), Plan(1, 9), Plan(SECOND - 1, 1, 1), Plan(FIRST - 1, 2), Plan(FIRST, 1), Plan(1, 2), Plan(SECOND, 1)]
+    return [
+        Plan(*[(2, 1)] * 4 + [(1, 1)] * 9),
+        Plan((SECOND - 1, 1)),
+        Plan((FIRST, FIRST), (FIRST - 1, FIRST - 1), (FIRST - 1, FIRST - 1)),
+        Plan((1, 1), (1, 1)),
+        Plan((SECOND, SECOND)),
+    ]
 
 
 def lane_pick(row, lo):
@@ -123,13 +110,13 @@
             device["gz"] = lax.rem(iz + nz - o[2], nz)
         return device
 
+    takes = [pltpu.make_async_copy(given[n], taken[n], take_sem.at[n]) for n in range(7)]
+    for n in (6, 0, 1, 2, 4, 5, 3):
+        takes[n].start()
     barrier = pltpu.get_barrier_semaphore()
     for o in offsets(SECOND):
         pl.semaphore_signal(barrier, inc=1, device_id=peer(o), device_id_type=MESH)
 
-    takes = [pltpu.make_async_copy(given[n], taken[n], take_sem.at[n]) for n in range(7)]
-    for n in (6, 0, 1, 2, 4, 5, 3):
-        takes[n].start()
     old_ref, new_ref, mass_ref, rest_ref, pair_ref, live_ref, send_ref = taken
 
     todo = plans()
@@ -144,16 +131,17 @@
     class Exchange:
         def __init__(self, number, levels):
             self.plan = plan = todo[number]
-            self.out, self.box, ssem, rsem = bufs[4 * number : 4 * number + 4]
-            for f, field in enumerate(levels):
-                for k, value in enumerate(field):
-                    for i in range(6):
-                        self.out[k, i, f : f + 1, :] = value[i : i + 1, :]
+            self.own = levels
+            out, self.box, ssem, rsem = bufs[4 * number : 4 * number + 4]
             self.copies = []
-            for n, (o, deep, row, count) in enumerate(plan.blocks):
+            for n, (o, start, count) in enumerate(plan.messages):
+                for (offset, k, i, f), row in plan.place.items():
+                    if offset == o:
+                        out[row] = levels[f][k - 1][i : i + 1, :]
+            for n, (o, start, count) in enumerate(plan.messages):
                 copy = pltpu.make_async_remote_copy(
-                    src_ref=self.out.at[pl.ds(0, deep), pl.ds(row, count)],
-                    dst_ref=self.box.at[plan.offsets.index(o), pl.ds(0, deep), pl.ds(row, count)],
+                    src_ref=out.at[pl.ds(start, count)],
+                    dst_ref=self.box.at[pl.ds(start, count)],
                     send_sem=ssem.at[n],
                     recv_sem=rsem.at[n],
                     device_id=peer(o),
@@ -168,8 +156,8 @@
 
         def row(self, o, k, i, f):
             if dist(o) == 0:
-                return self.out[k - 1, i, f : f + 1, :]
-            return self.box[self.plan.offsets.index(o), k - 1, i, f : f + 1, :]
+                return self.own[f][k - 1][i : i + 1, :]
+            return self.box[self.plan.place[o, k, i, f]]
 
         def faces(self, f):
             return [self.row(moved_by((0, 0, 0), i), 1, i, f) for i in range(6)]
@@ -299,9 +287,8 @@
     at_far = Index(jnp.where(face_rest > 0, far_atom, -1))
     far_fields = [at_far.look(field) for field in own_rows] + [face_rest, leaves.astype(F32)]
     pl.semaphore_wait(barrier, len(offsets(SECOND)))
-    nears = Exchange(0, [[field] for field in packed])
-    fars = Exchange(1, [[field] for field in far_fields])
-    pointers = Exchange(2, [[leaves.astype(F32)]])
+    atoms = Exchange(0, [[field] for field in packed + far_fields])
+    pointers = Exchange(1, [[leaves.astype(F32)]])
 
     def at_faces(field, depth=1):
         rows = rows_of(field)
@@ -333,9 +320,9 @@
     headed = contract(jnp.concatenate(heads, 0), low)
     head_code = (headed[0:8] + 128.0 * headed[8:16]).astype(I32)
 
-    nears.wait()
+    atoms.wait()
     at_ghost = [Index(jnp.where(remote, ghost + half, -1)) for half in (0, 64)]
-    from_second = [at_ghost[f // 4].look(nears.faces(f % 4), 8, from_second[f]) for f in range(7)]
+    from_second = [at_ghost[f // 4].look(atoms.faces(f % 4), 8, from_second[f]) for f in range(7)]
     span = [from_first[f] - from_second[f] for f in range(6)]
     mass1, mass2 = from_first[6], from_second[6]
     scale = jnp.where(alive, 1.0, 0.0) / jnp.sqrt(mass1 + mass2)
@@ -362,16 +349,15 @@
     diag_levels = at_faces(diag, SECOND - 1)
 
     here = (0, 0, 0)
-    arrived = [nears.arrived(here, 1, f) for f in range(4)]
+    arrived = [atoms.arrived(here, 1, f) for f in range(4)]
     near_atom = [
         jnp.where(lane < 64, arrived[f] if f < 4 else pltpu.roll(arrived[f - 4], 64, axis=1), across(fields[f])) for f in range(7)
     ]
-    fars.wait()
-    far_atom = [fars.arrived(here, 1, f) for f in range(8)]
-    leave = fars.arrived(here, 1, 8).astype(I32)
+    far_atom = [atoms.arrived(here, 1, 4 + f) for f in range(8)]
+    leave = atoms.arrived(here, 1, 12).astype(I32)
     leave_lane = leave & 127
     leave_row = jnp.where(leave_lane < 64, leave >> 7, -1)
-    seen = {v: [nears.arrived(v, 1, f) for f in range(4)] for v in offsets(1)}
+    seen = {v: [atoms.arrived(v, 1, f) for f in range(4)] for v in offsets(1)}
     for f in range(4):
         slot_ref = fresh("pile", pile_ref)
         for i in range(6):
@@ -413,15 +399,13 @@
     y = x
     y_ghost = x_ghost
     x, _ = step(x, x1, x2, [y_ghost], None, None)
-    moving = Exchange(4, [at_faces(x, FIRST)])
-    tables = Exchange(3, [diag_levels[: FIRST - 1], onward[: FIRST - 1]])
+    moving = Exchange(2, [at_faces(x, FIRST), diag_levels[: FIRST - 1], onward[: FIRST - 1]])
     x1, x2 = near(x)
     pointers.wait()
     exits = {v: Index(pointers.arrived(v, 1, 0).astype(I32)) for v in [(0, 0, 0)] + offsets(SECOND - 2)}
-    tables.wait()
-    diag_ghosts = tables.ghosts(0, FIRST - 1, exits)
-    link_ghosts = [inward] + tables.ghosts(1, FIRST - 1, exits)
     moving.wait()
+    diag_ghosts = moving.ghosts(1, FIRST - 1, exits)
+    link_ghosts = [inward] + moving.ghosts(2, FIRST - 1, exits)
     ghosts = moving.ghosts(0, FIRST, exits)
     for n in range(ORDER):
         y = y + x
@@ -438,7 +422,7 @@
             value = at_exit.look(rows_of(ghost_levels[SECOND - 2 - t], 6), 8 * t, value)
         return value
 
-    last = Exchange(5, [[resolved(diag_levels[-1], diag_ghosts)], [resolved(onward[-1], link_ghosts[1:])]])
+    last = Exchange(3, [[resolved(diag_levels[-1], diag_ghosts)], [resolved(onward[-1], link_ghosts[1:])]])
     y1, y2 = near(y)
     rows = rows_of(y_ghost, 6)
     y1 = at_n1.look(rows, 8, y1)
@@ -447,7 +431,7 @@
     square = rest * rest
     goal = jnp.sqrt(jnp.maximum(2.0 * square - dot3(stretch, stretch), 0.25 * square))
     x = scale * (rest - goal)
-    moving = Exchange(6, [at_faces(x, SECOND)])
+    moving = Exchange(4, [at_faces(x, SECOND)])
 
     x1, x2 = near(x)
     last.wait()

time: 37.3 us -> 35.7 us (0.957)
  Pallas kernels: 35.4 us -> 33.7 us
    pallas_call x1, Pallas kernels: 35.4 us -> 33.7 us  [per_device(): pl.pallas_call(kernel, out_shape=(pltpu.VMEM((3, 1024), F32), pltpu.VMEM(...]
where the time goes in v5:
time: 35.7 us; the launch traced here: 35.6 us
  Pallas kernels  33.7 us (94%)
  local copies, waits for them, and re-layouts  1.2 us (3%)
  between operations  0.64 us (2%)
    pallas_call x1, Pallas kernels, per_device(): pl.pallas_call(kernel, out_shape=(pltpu.VMEM((3, 1024), F32), pltpu.VMEM(...  33.7 us
    unnamed x2, local copies, waits for them, and re-layouts  1.2 us

profile of v5, /device:TPU:1, one launch (start us, length us, event | category | flops | bytes accessed | tf_op | source)
XLA Modules:
  0.0 35.6 jit_solution(9194234298022563737)
XLA Ops:
  0.6 33.7 %plincs.1 = (f32[3,1024]{1,0:T(4,128)S(1)}, f32[8,128]{1,0:T(8,128)S(1)}) custom-call(f32[3,1024]{1,0:T(4,128)} %refs_0_.1, f32[3,1024]{1,0:T(4,128)} %refs_1_.1, f32[8,128]{1,0:T(8,128)} %bitcast.5, f32[8,128]{1,0:T(8,128)} %bitcast.6, s32[2,1024]{1,0:T(2,128)} %refs_4_.1, s32[8,128]{1,0:T(8,128)} %bitcast.7, s32[6,48]{1,0:T(8,128)} %refs_6_.1), custom_call_target="tpu_custom_call" | custom-call | tf_op jit(solution)/shard_map/plincs/pallas_call | solution.py:479
  34.4 0.6 %copy.11 = f32[3,1024]{1,0:T(4,128)} copy(f32[3,1024]{1,0:T(4,128)S(1)} %get-tuple-element.6) | data formatting | bytes 24576
  35.0 0.6 %copy.12 = f32[1024]{0:T(1024)} copy(f32[1024]{0:T(1024)S(1)} %bitcast.4) | data formatting | bytes 8192

commit v6 on v5

--- a/solution.py
+++ b/solution.py
@@ -33,7 +33,7 @@
 class Plan:
     def __init__(self, *fields):
         self.messages, self.place, self.rows = [], {}, 0
-        for o in offsets(max(depth for depth, _ in fields)):
+        for o in sorted(offsets(max(depth for depth, _ in fields)), key=lambda o: -dist(o)):
             start = self.rows
             for f, (depth, levels) in enumerate(fields):
                 for i in range(6):
@@ -53,8 +53,7 @@
         Plan(*[(2, 1)] * 4 + [(1, 1)] * 9),
         Plan((SECOND - 1, 1)),
         Plan((FIRST, FIRST), (FIRST - 1, FIRST - 1), (FIRST - 1, FIRST - 1)),
-        Plan((1, 1), (1, 1)),
-        Plan((SECOND, SECOND)),
+        Plan((SECOND, SECOND), (1, 1), (1, 1)),
     ]
 
 
@@ -163,10 +162,10 @@
             return [self.row(moved_by((0, 0, 0), i), 1, i, f) for i in range(6)]
 
         def arrived(self, v, k, f):
-            slot_ref = fresh("tile", tile_ref, 6)
-            for i in range(6):
-                slot_ref[i : i + 1, :] = self.row(moved_by(v, i), k, i, f)
-            return slot_ref[...]
+            out = jnp.broadcast_to(self.row(moved_by(v, 0), k, 0, f), (8, 128))
+            for i in range(1, 6):
+                out = jnp.where(sub == i, self.row(moved_by(v, i), k, i, f), out)
+            return out
 
         def ghosts(self, f, depth, exits):
             here = [(0, 0, 0)] + offsets(depth - 1)
@@ -320,6 +319,21 @@
     headed = contract(jnp.concatenate(heads, 0), low)
     head_code = (headed[0:8] + 128.0 * headed[8:16]).astype(I32)
 
+    has_head = head_code > 0
+    head_first = head_code >= 4096
+    head_slot = (head_code & 4095) - 1
+    link = jnp.concatenate(link_rows, 0) - 1
+    at_head = Index(head_slot)
+    next1 = at_head.look(rows_of(n1))
+    next2 = at_head.look(rows_of(n2))
+    turn = jnp.where(head_first, 1.0, -1.0)
+    tail_slot = jnp.where(has_head, jnp.where(head_first, next1, next2), link)
+    at_tail = Index(tail_slot)
+    tail_sign = jnp.where(
+        head_first, at_head.look(rows_of(sign1)), at_head.look(rows_of(sign2))
+    )
+    crossed = [across(fields[f]) for f in range(7)]
+
     atoms.wait()
     at_ghost = [Index(jnp.where(remote, ghost + half, -1)) for half in (0, 64)]
     from_second = [at_ghost[f // 4].look(atoms.faces(f % 4), 8, from_second[f]) for f in range(7)]
@@ -351,7 +365,7 @@
     here = (0, 0, 0)
     arrived = [atoms.arrived(here, 1, f) for f in range(4)]
     near_atom = [
-        jnp.where(lane < 64, arrived[f] if f < 4 else pltpu.roll(arrived[f - 4], 64, axis=1), across(fields[f])) for f in range(7)
+        jnp.where(lane < 64, arrived[f] if f < 4 else pltpu.roll(arrived[f - 4], 64, axis=1), crossed[f]) for f in range(7)
     ]
     far_atom = [atoms.arrived(here, 1, 4 + f) for f in range(8)]
     leave = atoms.arrived(here, 1, 12).astype(I32)
@@ -422,7 +436,7 @@
             value = at_exit.look(rows_of(ghost_levels[SECOND - 2 - t], 6), 8 * t, value)
         return value
 
-    last = Exchange(3, [[resolved(diag_levels[-1], diag_ghosts)], [resolved(onward[-1], link_ghosts[1:])]])
+    relayed = [[resolved(diag_levels[-1], diag_ghosts)], [resolved(onward[-1], link_ghosts[1:])]]
     y1, y2 = near(y)
     rows = rows_of(y_ghost, 6)
     y1 = at_n1.look(rows, 8, y1)
@@ -431,13 +445,14 @@
     square = rest * rest
     goal = jnp.sqrt(jnp.maximum(2.0 * square - dot3(stretch, stretch), 0.25 * square))
     x = scale * (rest - goal)
-    moving = Exchange(4, [at_faces(x, SECOND)])
+    moving = Exchange(3, [at_faces(x, SECOND)] + relayed)
 
     x1, x2 = near(x)
-    last.wait()
-    diag_ghosts = diag_ghosts + [last.arrived((0, 0, 0), 1, 0)]
-    link_ghosts = link_ghosts + [last.arrived((0, 0, 0), 1, 1)]
+    arm_head = [turn * at_head.look(arm_rows[n]) for n in range(3)]
+    arm_tail = [at_tail.look(arm_ghosts[n], 8, tail_sign * at_tail.look(arm_rows[n])) for n in range(3)]
     moving.wait()
+    diag_ghosts = diag_ghosts + [moving.arrived(here, 1, 1)]
+    link_ghosts = link_ghosts + [moving.arrived(here, 1, 2)]
     ghosts = moving.ghosts(0, SECOND, exits)
     z, z_ghost = y, y_ghost
     for n in range(ORDER + 1):
@@ -450,21 +465,6 @@
     mult_ref[...] = z
 
     z_rows = rows_of(z)
-    has_head = head_code > 0
-    head_first = head_code >= 4096
-    head_slot = (head_code & 4095) - 1
-    link = jnp.concatenate(link_rows, 0) - 1
-    at_head = Index(head_slot)
-    next1 = at_head.look(rows_of(n1))
-    next2 = at_head.look(rows_of(n2))
-    turn = jnp.where(head_first, 1.0, -1.0)
-    tail_slot = jnp.where(has_head, jnp.where(head_first, next1, next2), link)
-    at_tail = Index(tail_slot)
-    tail_sign = jnp.where(
-        head_first, at_head.look(rows_of(sign1)), at_head.look(rows_of(sign2))
-    )
-    arm_head = [turn * at_head.look(arm_rows[n]) for n in range(3)]
-    arm_tail = [at_tail.look(arm_ghosts[n], 8, tail_sign * at_tail.look(arm_rows[n])) for n in range(3)]
     z_head = at_head.look(z_rows)
     z_tail = at_tail.look(z_rows)
     z_tail = at_tail.look(rows_of(z_ghost, 6), 8, z_tail)

time: 35.7 us -> 35.4 us (level)
  no operation moved by 1% of the time
where the time goes in v6:
time: 35.4 us; the launch traced here: 35.3 us
  Pallas kernels  33.4 us (94%)
  local copies, waits for them, and re-layouts  1.2 us (3%)
  between operations  0.64 us (2%)
    pallas_call x1, Pallas kernels, per_device(): pl.pallas_call(kernel, out_shape=(pltpu.VMEM((3, 1024), F32), pltpu.VMEM(...  33.4 us
    unnamed x2, local copies, waits for them, and re-layouts  1.2 us

profile of v6, /device:TPU:1, one launch (start us, length us, event | category | flops | bytes accessed | tf_op | source)
XLA Modules:
  0.0 35.3 jit_solution(15687097478919266720)
XLA Ops:
  0.6 33.4 %plincs.1 = (f32[3,1024]{1,0:T(4,128)S(1)}, f32[8,128]{1,0:T(8,128)S(1)}) custom-call(f32[3,1024]{1,0:T(4,128)} %refs_0_.1, f32[3,1024]{1,0:T(4,128)} %refs_1_.1, f32[8,128]{1,0:T(8,128)} %bitcast.5, f32[8,128]{1,0:T(8,128)} %bitcast.6, s32[2,1024]{1,0:T(2,128)} %refs_4_.1, s32[8,128]{1,0:T(8,128)} %bitcast.7, s32[6,48]{1,0:T(8,128)} %refs_6_.1), custom_call_target="tpu_custom_call" | custom-call | tf_op jit(solution)/shard_map/plincs/pallas_call | solution.py:479
  34.1 0.6 %copy.11 = f32[3,1024]{1,0:T(4,128)} copy(f32[3,1024]{1,0:T(4,128)S(1)} %get-tuple-element.6) | data formatting | bytes 24576
  34.7 0.6 %copy.12 = f32[1024]{0:T(1024)} copy(f32[1024]{0:T(1024)S(1)} %bitcast.4) | data formatting | bytes 8192

commit v7 on v6

--- a/solution.py
+++ b/solution.py
@@ -399,11 +399,13 @@
     onward = [jnp.where(end, at.look(e2_rows), at.look(e1_rows)) for at, end in zip(at_level[: SECOND - 1], ends)]
     inward = across(jnp.where(ends[0], at_level[0].look(e1_rows), at_level[0].look(e2_rows)))
 
+    at_cross = Index(across(face))
+
     def step(x, x1, x2, ghosts, diag_ghosts, link_ghosts):
         rows = rows_of(ghosts[0], 6)
         x1 = at_n1.look(rows, 8, x1)
         x2 = at_n2.look(rows, 8, x2)
-        chain = [across(at_faces(x)[0]) if len(ghosts) > 1 else None] + ghosts
+        chain = [at_cross.look(rows_of(x)) if len(ghosts) > 1 else None] + ghosts
         ghosts = [
             diag_ghosts[k - 1] * chain[k] + link_ghosts[k - 1] * chain[k - 1] + link_ghosts[k] * chain[k + 1]
             for k in range(1, len(chain) - 1)

time: 35.4 us -> 35.3 us (level)
  no operation moved by 1% of the time
where the time goes in v7:
time: 35.3 us; the launch traced here: 35.1 us
  Pallas kernels  33.3 us (94%)
  local copies, waits for them, and re-layouts  1.2 us (3%)
  between operations  0.64 us (2%)
    pallas_call x1, Pallas kernels, per_device(): pl.pallas_call(kernel, out_shape=(pltpu.VMEM((3, 1024), F32), pltpu.VMEM(...  33.3 us
    unnamed x2, local copies, waits for them, and re-layouts  1.2 us

profile of v7, /device:TPU:1, one launch (start us, length us, event | category | flops | bytes accessed | tf_op | source)
XLA Modules:
  0.0 35.1 jit_solution(16911175644408522204)
XLA Ops:
  0.6 33.3 %plincs.1 = (f32[3,1024]{1,0:T(4,128)S(1)}, f32[8,128]{1,0:T(8,128)S(1)}) custom-call(f32[3,1024]{1,0:T(4,128)} %refs_0_.1, f32[3,1024]{1,0:T(4,128)} %refs_1_.1, f32[8,128]{1,0:T(8,128)} %bitcast.5, f32[8,128]{1,0:T(8,128)} %bitcast.6, s32[2,1024]{1,0:T(2,128)} %refs_4_.1, s32[8,128]{1,0:T(8,128)} %bitcast.7, s32[6,48]{1,0:T(8,128)} %refs_6_.1), custom_call_target="tpu_custom_call" | custom-call | tf_op jit(solution)/shard_map/plincs/pallas_call | solution.py:481
  33.9 0.6 %copy.11 = f32[3,1024]{1,0:T(4,128)} copy(f32[3,1024]{1,0:T(4,128)S(1)} %get-tuple-element.6) | data formatting | bytes 24576
  34.5 0.6 %copy.12 = f32[1024]{0:T(1024)} copy(f32[1024]{0:T(1024)S(1)} %bitcast.4) | data formatting | bytes 8192
